TPU v7x, 32 devices: a whole 2x2x4 slice. The times are simulated.
32 devices in a mesh: gy: 8 (over z, x), gx: 4 (over y, core).
Axes of the slice: x: 2, y: 2, z: 4, core: 2. Of those that a mesh axis runs over, the one named last changes fastest.
Arguments:
- imbalance: float32 [4, 1024, 2048], P(None, 'gy', 'gx'), may hold values from -9 to 9
- flow: float32 [2, 4, 1024, 2048], P(None, None, 'gy', 'gx'), may hold values from -3 to 3
- potential: float32 [4, 1024, 2048], P(None, 'gy', 'gx'), may hold values from -5 to 5
- cost: float32 [1024, 2048], P('gy', 'gx'), may hold values from 0.2 to 2
Outputs:
- flow_out: float32 [2, 4, 1024, 2048], P(None, None, 'gy', 'gx')
- potential_out: float32 [4, 1024, 2048], P(None, 'gy', 'gx')
- residual: float32 [4], replicated
All inputs are finite; a program needn't handle non-finite values.
Results may differ from a plain program's by a relative error of at most 0.0001.
Values sent between devices are 32-bit elements; how exact they have to be, the bound alone decides.
A program may use at most 64 MiB of HBM per device.

v0:
```python
import jax
import jax.numpy as jnp
from jax import lax
from jax.sharding import PartitionSpec as P

ITERS = 12


initial_step = 0.35
epsilon = 1e-06


def shifted(value, axis, steps):
    count = lax.axis_size(axis)
    leading, last = (max(0, -steps), min(count, count - steps))
    return lax.ppermute(value, axis, [(source, source + steps) for source in range(leading, last)])


def gradient(potential):
    from_below = shifted(potential[:, 0, :], "gy", -1)
    from_right = shifted(potential[:, :, 0], "gx", -1)
    slope_down = jnp.concatenate([potential[:, 1:, :], from_below[:, None, :]], 1) - potential
    slope_right = jnp.concatenate([potential[:, :, 1:], from_right[:, :, None]], 2) - potential
    return (slope_down, slope_right)


def divergence(flow_down, flow_right):
    from_above = shifted(flow_down[:, -1, :], "gy", 1)
    from_left = shifted(flow_right[:, :, -1], "gx", 1)
    above_rows = jnp.concatenate([from_above[:, None, :], flow_down[:, :-1, :]], 1)
    left_cols = jnp.concatenate([from_left[:, :, None], flow_right[:, :, :-1]], 2)
    return flow_down - above_rows + flow_right - left_cols


def shrink(moved_down, moved_right, threshold):
    magnitude = jnp.sqrt(moved_down * moved_down + moved_right * moved_right)
    factor = jnp.maximum(magnitude - threshold, 0.0) / jnp.maximum(magnitude, threshold)
    return (factor * moved_down, factor * moved_right)


def local(imbalance, flow, potential, cost):
    local_rows, local_cols = cost.shape

    def primal(flow_down, flow_right, field, spread_old, primal_rate):
        slope_down, slope_right = gradient(field)
        rate_now = primal_rate[:, None, None]
        new_down, new_right = shrink(
            flow_down + rate_now * slope_down,
            flow_right + rate_now * slope_right,
            rate_now * cost[None],
        )
        return (new_down, new_right, spread_old, None)

    spread_start = divergence(flow[0], flow[1])

    def iterate(carried, with_stats):
        flow_down, flow_right, field, spread_old, primal_rate, dual_rate = carried
        new_down, new_right, spread_old, spread_new = primal(
            flow_down, flow_right, field, spread_old, primal_rate
        )
        if with_stats:
            diff_down = new_down - flow_down
            diff_right = new_right - flow_right
            primal_local = jnp.sum(diff_down * diff_down + diff_right * diff_right, axis=(1, 2))
        spread_new = divergence(new_down, new_right)
        new_field = field + dual_rate[:, None, None] * (2.0 * spread_new - spread_old - imbalance)
        if with_stats:
            change = new_field - field
            dual_local = jnp.sum(change * change, axis=(1, 2))
            primal_change, dual_change = lax.psum((primal_local, dual_local), ("gy", "gx"))
            rescale = jnp.sqrt(jnp.sqrt((primal_change + epsilon) / (dual_change + epsilon)))
            primal_rate = primal_rate / rescale
            dual_rate = dual_rate * rescale
        return (new_down, new_right, new_field, spread_new, primal_rate, dual_rate)

    def loop_turn(counter, carried):
        return iterate(carried, True)

    starting = jnp.full((potential.shape[0],), initial_step, jnp.float32)
    carried = (flow[0], flow[1], potential, spread_start, starting, starting)
    carried = lax.fori_loop(0, ITERS - 1, loop_turn, carried)
    closing = iterate(carried, False)
    shortfall = closing[3] - imbalance
    total_sum = lax.psum(jnp.sum(shortfall * shortfall, axis=(1, 2)), ("gy", "gx"))
    cell_count = local_rows * lax.axis_size("gy") * local_cols * lax.axis_size("gx")
    residual = total_sum / cell_count
    return (jnp.stack([closing[0], closing[1]]), closing[2], residual)


def solution(mesh):
    placed = (P(None, "gy", "gx"), P(None, None, "gy", "gx"), P(None, "gy", "gx"), P("gy", "gx"))
    return jax.shard_map(
        local,
        mesh=mesh,
        in_specs=placed,
        out_specs=(P(None, None, "gy", "gx"), P(None, "gy", "gx"), P()),
        check_vma=False,
    )
```

profile of v0, /device:TPU:0, one launch (start us, length us, event | category | flops | bytes accessed | tf_op | source)
XLA Modules:
  0.0 887.7 jit_solution(16072063486011655081)
XLA Ops:
  3.7 4.9 collective-permute-start.4
  13.2 2.5 copy.72
  18.1 3.4 fusion.12
  21.5 791.1 %while.21 = (s32[]{:T(128)}, f32[4,128,512]{1,0,2:T(4,128)S(1)}, f32[4,128,512]{1,0,2:T(4,128)S(1)}, f32[4,128,512]{1,0,2:T(4,128)S(1)}, f32[4,128,512]{1,0,2:T(...) while((s32[]{:T(128)}, f32[4,128,512]{1,0,2:T(4,128)S(1)}, ...), condition=%wide.region_5.0_spmd.clone, body=%wide.region_0.0_spmd.clone.sunk | while | flops 10747943 | bytes 36053636 | solution.py:81
  30.0 3.8 fusion.33
  38.4 4.4 collective-permute-start.3
  42.7 3.2 collective-permute-start.2
  48.4 5.4 multiply_reduce_fusion.3
  53.8 42.1 %all-reduce.2 = (f32[4]{0:T(128)S(1)}, f32[4]{0:T(128)S(1)}) all-reduce(f32[4]{0:T(128)S(1)} %get-tuple-element.228, f32[4]{0:T(128)S(1)} %get-tuple-element.229), channel_id=1, replica_groups=mesh['gy'=8,'gx'=4] {'gy','gx'}, use_global_device_ids=true, to_apply=%region_4.0 | all-reduce | flops 8 | bytes 64 | tf_op jit(solution)/shard_map/while/body/eval_jaxpr/psum | solution.py:70
  101.6 1.8 collective-permute-done.1
  104.8 3.8 fusion.33
  113.1 4.8 collective-permute-start.3
  122.2 5.4 multiply_reduce_fusion.3
  127.5 39.6 %all-reduce.2 = (f32[4]{0:T(128)S(1)}, f32[4]{0:T(128)S(1)}) all-reduce(f32[4]{0:T(128)S(1)} %get-tuple-element.228, f32[4]{0:T(128)S(1)} %get-tuple-element.229), channel_id=1, replica_groups=mesh['gy'=8,'gx'=4] {'gy','gx'}, use_global_device_ids=true, to_apply=%region_4.0 | all-reduce | flops 8 | bytes 64 | tf_op jit(solution)/shard_map/while/body/eval_jaxpr/psum | solution.py:70
  172.9 1.8 collective-permute-done.1
  176.1 3.8 fusion.33
  184.4 4.8 collective-permute-start.3
  193.4 5.4 multiply_reduce_fusion.3
  198.8 40.4 %all-reduce.2 = (f32[4]{0:T(128)S(1)}, f32[4]{0:T(128)S(1)}) all-reduce(f32[4]{0:T(128)S(1)} %get-tuple-element.228, f32[4]{0:T(128)S(1)} %get-tuple-element.229), channel_id=1, replica_groups=mesh['gy'=8,'gx'=4] {'gy','gx'}, use_global_device_ids=true, to_apply=%region_4.0 | all-reduce | flops 8 | bytes 64 | tf_op jit(solution)/shard_map/while/body/eval_jaxpr/psum | solution.py:70
  245.0 1.8 collective-permute-done.1
  248.1 3.8 fusion.33
  256.4 4.8 collective-permute-start.3
  265.5 5.4 multiply_reduce_fusion.3
  270.9 39.6 %all-reduce.2 = (f32[4]{0:T(128)S(1)}, f32[4]{0:T(128)S(1)}) all-reduce(f32[4]{0:T(128)S(1)} %get-tuple-element.228, f32[4]{0:T(128)S(1)} %get-tuple-element.229), channel_id=1, replica_groups=mesh['gy'=8,'gx'=4] {'gy','gx'}, use_global_device_ids=true, to_apply=%region_4.0 | all-reduce | flops 8 | bytes 64 | tf_op jit(solution)/shard_map/while/body/eval_jaxpr/psum | solution.py:70
  316.2 1.8 collective-permute-done.1
  319.4 3.8 fusion.33
  327.7 4.8 collective-permute-start.3
  336.7 5.4 multiply_reduce_fusion.3
  342.1 40.4 %all-reduce.2 = (f32[4]{0:T(128)S(1)}, f32[4]{0:T(128)S(1)}) all-reduce(f32[4]{0:T(128)S(1)} %get-tuple-element.228, f32[4]{0:T(128)S(1)} %get-tuple-element.229), channel_id=1, replica_groups=mesh['gy'=8,'gx'=4] {'gy','gx'}, use_global_device_ids=true, to_apply=%region_4.0 | all-reduce | flops 8 | bytes 64 | tf_op jit(solution)/shard_map/while/body/eval_jaxpr/psum | solution.py:70
  388.3 1.8 collective-permute-done.1
  391.5 3.8 fusion.33
  399.8 4.8 collective-permute-start.3
  408.8 5.4 multiply_reduce_fusion.3
  414.2 39.6 %all-reduce.2 = (f32[4]{0:T(128)S(1)}, f32[4]{0:T(128)S(1)}) all-reduce(f32[4]{0:T(128)S(1)} %get-tuple-element.228, f32[4]{0:T(128)S(1)} %get-tuple-element.229), channel_id=1, replica_groups=mesh['gy'=8,'gx'=4] {'gy','gx'}, use_global_device_ids=true, to_apply=%region_4.0 | all-reduce | flops 8 | bytes 64 | tf_op jit(solution)/shard_map/while/body/eval_jaxpr/psum | solution.py:70
  462.7 3.8 fusion.33
  471.0 4.8 collective-permute-start.3
  480.1 5.4 multiply_reduce_fusion.3
  485.5 40.4 %all-reduce.2 = (f32[4]{0:T(128)S(1)}, f32[4]{0:T(128)S(1)}) all-reduce(f32[4]{0:T(128)S(1)} %get-tuple-element.228, f32[4]{0:T(128)S(1)} %get-tuple-element.229), channel_id=1, replica_groups=mesh['gy'=8,'gx'=4] {'gy','gx'}, use_global_device_ids=true, to_apply=%region_4.0 | all-reduce | flops 8 | bytes 64 | tf_op jit(solution)/shard_map/while/body/eval_jaxpr/psum | solution.py:70
  534.8 3.8 fusion.33
  543.1 4.8 collective-permute-start.3
  552.1 5.4 multiply_reduce_fusion.3
  557.5 39.6 %all-reduce.2 = (f32[4]{0:T(128)S(1)}, f32[4]{0:T(128)S(1)}) all-reduce(f32[4]{0:T(128)S(1)} %get-tuple-element.228, f32[4]{0:T(128)S(1)} %get-tuple-element.229), channel_id=1, replica_groups=mesh['gy'=8,'gx'=4] {'gy','gx'}, use_global_device_ids=true, to_apply=%region_4.0 | all-reduce | flops 8 | bytes 64 | tf_op jit(solution)/shard_map/while/body/eval_jaxpr/psum | solution.py:70
  602.9 1.8 collective-permute-done.1
  606.0 3.8 fusion.33
  614.3 4.8 collective-permute-start.3
  623.4 5.4 multiply_reduce_fusion.3
  628.8 40.4 %all-reduce.2 = (f32[4]{0:T(128)S(1)}, f32[4]{0:T(128)S(1)}) all-reduce(f32[4]{0:T(128)S(1)} %get-tuple-element.228, f32[4]{0:T(128)S(1)} %get-tuple-element.229), channel_id=1, replica_groups=mesh['gy'=8,'gx'=4] {'gy','gx'}, use_global_device_ids=true, to_apply=%region_4.0 | all-reduce | flops 8 | bytes 64 | tf_op jit(solution)/shard_map/while/body/eval_jaxpr/psum | solution.py:70
  675.0 1.8 collective-permute-done.1
  678.1 3.8 fusion.33
  686.4 4.8 collective-permute-start.3
  695.5 5.4 multiply_reduce_fusion.3
  700.9 39.6 %all-reduce.2 = (f32[4]{0:T(128)S(1)}, f32[4]{0:T(128)S(1)}) all-reduce(f32[4]{0:T(128)S(1)} %get-tuple-element.228, f32[4]{0:T(128)S(1)} %get-tuple-element.229), channel_id=1, replica_groups=mesh['gy'=8,'gx'=4] {'gy','gx'}, use_global_device_ids=true, to_apply=%region_4.0 | all-reduce | flops 8 | bytes 64 | tf_op jit(solution)/shard_map/while/body/eval_jaxpr/psum | solution.py:70
  746.2 1.8 collective-permute-done.1
  749.4 3.8 fusion.33
  757.7 4.8 collective-permute-start.3
  766.7 5.4 multiply_reduce_fusion.3
  772.1 40.4 %all-reduce.2 = (f32[4]{0:T(128)S(1)}, f32[4]{0:T(128)S(1)}) all-reduce(f32[4]{0:T(128)S(1)} %get-tuple-element.228, f32[4]{0:T(128)S(1)} %get-tuple-element.229), channel_id=1, replica_groups=mesh['gy'=8,'gx'=4] {'gy','gx'}, use_global_device_ids=true, to_apply=%region_4.0 | all-reduce | flops 8 | bytes 64 | tf_op jit(solution)/shard_map/while/body/eval_jaxpr/psum | solution.py:70
  817.1 2.5 slice.98
  825.9 2.8 fusion.20
  829.6 3.0 collective-permute-start.9
  832.6 4.8 collective-permute-start.8
  839.1 2.7 multiply_reduce_fusion.1
  841.9 42.0 %psum.21 = f32[4]{0:T(128)S(1)} all-reduce(f32[4]{0:T(128)S(1)} %get-tuple-element.148), channel_id=1, replica_groups=mesh['gy'=8,'gx'=4] {'gy','gx'}, use_global_device_ids=true, to_apply=%region_7.0 | all-reduce | flops 4 | bytes 32 | tf_op jit(solution)/shard_map/psum | solution.py:84
  884.3 3.3 multiply_add_fusion.1
  (303 shorter events, 199.6 us)
Async XLA Ops:
  3.7 13.1 %collective-permute-start.4 = (f32[4,512]{1,0:T(4,128)S(1)}, f32[4,512]{1,0:T(4,128)S(1)}, u32[]{:S(2)}, u32[]{:S(2)}) collective-permute-start(f32[4,512]{1,0:T(4,128)S(1)} %bitcast.78), channel_id=1, source_target_pairs={{0,4},{4,8},{8,12},{12,16},{16,20},{20,24},{24,28},{1,5},{5,9},{9,... | collective-permute-start | bytes 24584 | tf_op jit(solution)/shard_map/ppermute | solution.py:16
  9.0 9.1 %collective-permute-start.5 = (f32[4,128]{1,0:T(4,128)S(1)}, f32[4,128]{1,0:T(4,128)S(1)}, u32[]{:S(2)}, u32[]{:S(2)}) collective-permute-start(f32[4,128]{1,0:T(4,128)S(1)} %slice_bitcast_fusion.2), channel_id=1, source_target_pairs={{0,1},{1,2},{2,3},{4,5},{5,6},{6,7},{8,9},{9,10},{10,11},{12,13},{... | collective-permute-start | bytes 6152 | tf_op jit(solution)/shard_map/ppermute | solution.py:16
  21.5 8.5 collective-permute-start
  23.1 5.5 collective-permute-start.1
  30.0 3.8 copy-start
  38.4 8.7 collective-permute-start.3
  42.7 5.7 collective-permute-start.2
  96.0 8.8 collective-permute-start
  97.6 5.8 collective-permute-start.1
  104.8 3.8 copy-start
  113.1 7.7 collective-permute-start.3
  117.9 4.2 collective-permute-start.2
  167.2 8.8 collective-permute-start
  168.9 5.8 collective-permute-start.1
  176.0 3.8 copy-start
  184.4 7.7 collective-permute-start.3
  189.2 4.2 collective-permute-start.2
  239.3 8.8 collective-permute-start
  241.0 5.8 collective-permute-start.1
  248.1 3.8 copy-start
  256.4 7.7 collective-permute-start.3
  261.3 4.2 collective-permute-start.2
  310.6 8.8 collective-permute-start
  312.2 5.8 collective-permute-start.1
  319.4 3.8 copy-start
  327.7 7.7 collective-permute-start.3
  332.5 4.2 collective-permute-start.2
  382.6 8.8 collective-permute-start
  384.3 5.8 collective-permute-start.1
  391.4 3.8 copy-start
  399.8 7.7 collective-permute-start.3
  404.6 4.2 collective-permute-start.2
  453.9 8.8 collective-permute-start
  455.5 5.8 collective-permute-start.1
  462.7 3.8 copy-start
  471.0 7.7 collective-permute-start.3
  475.9 4.2 collective-permute-start.2
  526.0 8.8 collective-permute-start
  527.6 5.8 collective-permute-start.1
  534.8 3.8 copy-start
  543.1 7.7 collective-permute-start.3
  547.9 4.2 collective-permute-start.2
  597.2 8.8 collective-permute-start
  598.9 5.8 collective-permute-start.1
  606.0 3.8 copy-start
  614.3 7.7 collective-permute-start.3
  619.2 4.2 collective-permute-start.2
  669.3 8.8 collective-permute-start
  671.0 5.8 collective-permute-start.1
  678.1 3.8 copy-start
  686.4 7.7 collective-permute-start.3
  691.3 4.2 collective-permute-start.2
  740.5 8.8 collective-permute-start
  742.2 5.8 collective-permute-start.1
  749.4 3.8 copy-start
  757.7 7.7 collective-permute-start.3
  762.5 4.2 collective-permute-start.2
  813.0 12.8 %collective-permute-start.6 = (f32[4,512]{1,0:T(4,128)S(1)}, f32[4,512]{1,0:T(4,128)S(1)}, u32[]{:S(2)}, u32[]{:S(2)}) collective-permute-start(f32[4,512]{1,0:T(4,128)S(1)} %bitcast.77), channel_id=1, source_target_pairs={{4,0},{8,4},{12,8},{16,12},{20,16},{24,20},{28,24},{5,1},{9,5},{13... | collective-permute-start | bytes 24584 | tf_op jit(solution)/shard_map/ppermute | solution.py:16
  814.3 10.7 %collective-permute-start.7 = (f32[4,128]{1,0:T(4,128)S(1)}, f32[4,128]{1,0:T(4,128)S(1)}, u32[]{:S(2)}, u32[]{:S(2)}) collective-permute-start(f32[4,128]{1,0:T(4,128)S(1)} %slice_bitcast_fusion.3), channel_id=1, source_target_pairs={{1,0},{2,1},{3,2},{5,4},{6,5},{7,6},{9,8},{10,9},{11,10},{13,12},{... | collective-permute-start | bytes 6152 | tf_op jit(solution)/shard_map/ppermute | solution.py:16
  820.9 2.7 copy-start.1
  822.3 3.6 copy-start.3
  822.3 3.6 copy-start.5
  829.6 9.4 %collective-permute-start.9 = (f32[4,128]{1,0:T(4,128)S(1)}, f32[4,128]{1,0:T(4,128)S(1)}, u32[]{:S(2)}, u32[]{:S(2)}) collective-permute-start(f32[4,128]{1,0:T(4,128)S(1)} %slice_reduce_fusion), channel_id=1, source_target_pairs={{0,1},{1,2},{2,3},{4,5},{5,6},{6,7},{8,9},{9,10},{10,11},{12,13},{... | collective-permute-start | bytes 6152 | tf_op jit(solution)/shard_map/ppermute | solution.py:16
  832.6 6.5 collective-permute-start.8
  (2 other events, 4.7 us)
where the time goes:
time: 891 us; the launch traced here: 888 us
  blocking collectives  484 us (54%)
  local copies, waits for them, and re-layouts  132 us (15%)
  other arithmetic  131 us (15%)
  starting transfers between devices  118 us (13%)
  waiting for transfers between devices  19.6 us (2%)
    psum x11, blocking collectives, iterate(): lax.psum((primal_local, dual_local), ('gy', 'gx'))  442 us
    ppermute x50, starting transfers between devices, shifted(): lax.ppermute(value, axis, [(source, source + steps) for source in range(l...  118 us
    reduce_sum x11, other arithmetic, iterate(): dual_local = jnp.sum(change * change, axis=(1, 2))  59.3 us
    div x11, other arithmetic, shrink(): jnp.maximum(magnitude - threshold, 0.0) / jnp.maximum(magnitude, threshold)  42.2 us
    psum x1, blocking collectives, local(): lax.psum(jnp.sum(shortfall * shortfall, axis=(1, 2)), ('gy', 'gx'))  42 us
    slice x25, local copies, waits for them, and re-layouts, divergence(): from_above = shifted(flow_down[:, -1, :], 'gy', 1)  35.4 us
    slice x12, local copies, waits for them, and re-layouts, gradient(): potential[:, 1:, :]  20.5 us
    ppermute x50, waiting for transfers between devices, shifted(): lax.ppermute(value, axis, [(source, source + steps) for source in range(l...  19.6 us
  transfers between devices with their start and end apart: 50, of which 11 were waited for; matrix products, arithmetic and copies ran while one was open for 11% of the time, Pallas kernels for 0%

commit v1 on v0

v1 whole, which is shorter than its diff:
```python
import functools

import jax
import jax.numpy as jnp
from jax import lax
from jax.experimental import pallas as pl
from jax.experimental.pallas import tpu as pltpu
from jax.sharding import PartitionSpec as P

ITERS = 12
LANES = 128
SUBS = 8

initial_step = 0.35
epsilon = 1e-06
MESH = pl.DeviceIdType.MESH


def kernel(
    ny, nx,
    imb_hbm, flow_hbm, u_hbm, cost_hbm,
    flow_hbm_out, u_hbm_out, res_out,
    imb_in, flow_in, u_in, cost_in,
    A, B, U, R, IM, CO,
    tau_ref, sig_ref,
    row_send, col_send, row_recv, col_recv, msg_send, msg_recv,
    ext_row, ext_col, ext_row_in, ext_col_in, grow, gcol,
    halo_ssem, halo_rsem, msg_ssem, msg_rsem, ext_ssem, ext_rsem, in_sem, out_sem,
):
    pairs, T, _, C = A.shape
    n = ny * nx
    gy, gx = lax.axis_index("gy"), lax.axis_index("gx")
    me = gy * nx + gx
    up, down, left, right = gy > 0, gy < ny - 1, gx > 0, gx < nx - 1
    f32 = jnp.float32

    K = C // LANES

    def column(ref, k):
        return ref.at[(slice(None),) * (len(ref.shape) - 1) + (pl.ds(k * LANES, LANES),)]

    fetches = [
        pltpu.make_async_copy(column(src, k), dst.at[k], in_sem.at[i, k])
        for i, (src, dst) in enumerate(((cost_hbm, cost_in), (u_hbm, u_in), (flow_hbm, flow_in), (imb_hbm, imb_in)))
        for k in range(K)
    ]
    for copy in fetches:
        copy.start()

    def gather(ref, *index):
        rows = pl.ds(index[-1], SUBS, stride=T)
        return jnp.concatenate([ref[(k,) + index[:-1] + (rows, slice(None))] for k in range(K)], axis=1)

    def scatter(ref, value, *index):
        rows = pl.ds(index[-1], SUBS, stride=T)
        for k in range(K):
            ref[(k,) + index[:-1] + (rows, slice(None))] = value[:, k * LANES:(k + 1) * LANES]

    barrier = pltpu.get_barrier_semaphore()

    def coords(offset):
        other = lax.rem(me + offset, n)
        return (other // nx, lax.rem(other, nx))

    def greet(k, c):
        pl.semaphore_signal(barrier, inc=1, device_id=coords(k), device_id_type=MESH)
        return c

    lax.fori_loop(1, n, greet, 0)

    lane = lax.broadcasted_iota(jnp.int32, (SUBS, LANES), 1)
    sub = lax.broadcasted_iota(jnp.int32, (SUBS, LANES), 0)
    subw = lax.broadcasted_iota(jnp.int32, (SUBS, C), 0)
    group, within = lane // T, lax.rem(lane, T)
    lane1, within1 = lane[0:1], within[0:1]

    def wide(x):
        return jnp.concatenate([x] * (C // LANES), axis=1)

    def row8(x, width):
        return jnp.broadcast_to(x, (SUBS, width))

    def to_left(x, entering):
        r = pltpu.roll(x, C - 1, 1)
        lanes = lax.broadcasted_iota(jnp.int32, entering.shape, 1)
        tail = jnp.where(lanes == LANES - 1, entering, r[:, C - LANES:])
        return jnp.concatenate([r[:, : C - LANES], tail], axis=1)

    def to_right(x, entering):
        r = pltpu.roll(x, 1, 1)
        head = jnp.where(lane == 0, entering, r[:, :LANES])
        return jnp.concatenate([head, r[:, LANES:]], axis=1)

    def pack_first(acc, x, t):
        v = x[:, :LANES]
        return jnp.where(lane == t, pltpu.roll(v, t, 1) if t else v, acc)

    def pack_last(acc, x, t):
        v = pltpu.roll(x[:, C - LANES:], (t + 1) % LANES, 1)
        return jnp.where(lane == t, v, acc)

    def place(acc, packed, p):
        return jnp.where(group == p, pltpu.roll(packed, p * T, 1), acc)

    def remote(src, dst, ssem, rsem, where):
        return pltpu.make_async_remote_copy(
            src_ref=src, dst_ref=dst, send_sem=ssem, recv_sem=rsem, device_id=where, device_id_type=MESH
        )

    def halos(slot):
        rows = [
            (ok_to, ok_from, remote(row_send.at[slot, k], row_recv.at[slot, k], halo_ssem.at[slot, k], halo_rsem.at[slot, k], (gy + d, gx)))
            for k, d, ok_to, ok_from in ((0, -1, up, down), (1, 1, down, up))
        ]
        cols = [
            (ok_to, ok_from, remote(col_send.at[slot, k], col_recv.at[slot, k], halo_ssem.at[slot, 2 + k], halo_rsem.at[slot, 2 + k], (gy, gx + d)))
            for k, d, ok_to, ok_from in ((0, -1, left, right), (1, 1, right, left))
        ]
        return rows + cols

    def extras():
        return [
            (down, up, remote(ext_row, ext_row_in, ext_ssem.at[0], ext_rsem.at[0], (gy + 1, gx))),
            (right, left, remote(ext_col, ext_col_in, ext_ssem.at[1], ext_rsem.at[1], (gy, gx + 1))),
        ]

    def start_all(copies):
        for ok_to, _, copy in copies:
            @pl.when(ok_to)
            def _(copy=copy):
                copy.start()

    def wait_all(copies):
        for ok_to, ok_from, copy in copies:
            @pl.when(ok_from)
            def _(copy=copy):
                copy.wait_recv()

            @pl.when(ok_to)
            def _(copy=copy):
                copy.wait_send()

    def send_message(slot, row):
        msg_send[slot] = row
        msg_recv[slot, me] = row

        def send(k, c):
            remote(msg_send.at[slot], msg_recv.at[slot, me], msg_ssem.at[slot], msg_rsem.at[slot], coords(k)).start()
            return c

        lax.fori_loop(1, n, send, 0)

    def wait_message(slot):
        whole = msg_recv.at[slot, pl.ds(0, n - 1)]
        pltpu.make_async_copy(whole, whole, msg_rsem.at[slot]).wait()
        pltpu.make_async_copy(whole, whole, msg_ssem.at[slot]).wait()

    def total_rows(slot):
        parts = [msg_recv[slot, k] for k in range(n)]
        while len(parts) > 1:
            parts = [sum(parts[k + 1:k + 2], parts[k]) for k in range(0, len(parts), 2)]
        total = row8(parts[0], LANES)
        pick = jnp.where(sub < pairs, sub * T + 1, (sub - pairs) * T + 2)
        return row8_lanes(jnp.sum(jnp.where(lane == pick, total, 0.0), axis=1, keepdims=True))

    def row8_lanes(x):
        return jnp.broadcast_to(x, (SUBS, LANES))

    def message(first, last, sums_a, sums_b):
        return jnp.where(
            within1 == T - 1, first[SUBS - 1:SUBS],
            jnp.where(within1 == 0, last[0:1], jnp.where(within1 == 1, sums_a, sums_b)),
        )

    ones = jnp.ones((SUBS, LANES), f32)
    for copy in fetches:
        copy.wait()
    for t in range(T):
        CO[t] = gather(cost_in, t)

    def load(p, carry):
        packs = [ones] * 5
        for t in range(T):
            a, b = gather(flow_in, 0, p, t), gather(flow_in, 1, p, t)
            u = gather(u_in, p, t)
            A[p, t] = a
            B[p, t] = b
            U[p, t] = u
            IM[p, t] = gather(imb_in, p, t)
            packs[0] = pack_first(packs[0], u, t)
            for k, x in ((1, u), (2, a), (3, b), (4, CO[t])):
                packs[k] = pack_last(packs[k], x, t)
            if t == 0:
                row_send[0, 0, pl.ds(p, 1), :] = u[0:1]
            if t == T - 1:
                row_send[0, 1, pl.ds(p, 1), :] = u[SUBS - 1:]
                ext_row[0, pl.ds(p, 1), :] = a[SUBS - 1:]
                ext_row[1, pl.ds(p, 1), :] = b[SUBS - 1:]
                ext_row[2, pl.ds(p, 1), :] = CO[t][SUBS - 1:]
        return tuple(place(c, x, p) for c, x in zip(carry, packs))

    first, last, last_a, last_b, last_c = lax.fori_loop(0, pairs, load, (ones,) * 5)
    col_send[0, 0] = first
    col_send[0, 1] = last
    ext_col[0] = last_a
    ext_col[1] = last_b
    ext_col[2] = last_c
    tau_ref[...] = jnp.full((SUBS, LANES), initial_step, f32)
    sig_ref[...] = jnp.full((SUBS, LANES), initial_step, f32)

    for missing, refs in (
        (jnp.logical_not(down), [row_recv.at[s, 0] for s in range(2)]),
        (jnp.logical_not(up), [row_recv.at[s, 1] for s in range(2)] + [ext_row_in]),
        (jnp.logical_not(right), [col_recv.at[s, 0] for s in range(2)]),
        (jnp.logical_not(left), [col_recv.at[s, 1] for s in range(2)] + [ext_col_in]),
    ):
        @pl.when(missing)
        def _(refs=refs):
            for ref in refs:
                ref[...] = jnp.zeros(ref.shape, f32)

    pl.semaphore_wait(barrier, n - 1)
    start_all(extras())
    start_all(halos(0))
    send_message(0, message(first, last, ones[0:1], ones[0:1]))
    wait_all(extras())
    grow[...] = ext_row_in[0:2]
    gcol[...] = ext_col_in[0:2]

    def above_first(a_last, p):
        ghost = row8(grow[0, pl.ds(p, 1), :], C)
        return jnp.where(subw == 0, ghost, pltpu.roll(a_last, 1, 0))

    def shortfall(p, t, a, a_above, b, gb):
        b_left = to_right(b, pltpu.roll(gb, (LANES - t) % LANES, 1))
        return ((a - a_above) + (b - b_left)) - IM[p, t]

    def ghost_flux(p):
        return pltpu.roll(gcol[1], lax.rem(LANES - p * T, LANES), 1)

    def begin(p, c):
        gb = ghost_flux(p)
        for t in range(T):
            above = A[p, t - 1] if t else above_first(A[p, T - 1], p)
            R[p, t] = shortfall(p, t, A[p, t], above, B[p, t], gb)
        return c

    lax.fori_loop(0, pairs, begin, 0)
    wait_all(halos(0))
    wait_message(0)

    results = [
        pltpu.make_async_copy(src.at[k], column(dst, k), out_sem.at[i, k])
        for i, (src, dst) in enumerate(((flow_in, flow_hbm_out), (u_in, u_hbm_out)))
        for k in range(K)
    ]

    def shrink(va, vb, t):
        f = jnp.maximum(1.0 - t * lax.rsqrt(va * va + vb * vb), 0.0)
        return f * va, f * vb

    def ghosts(slot):
        u = row_recv[slot, 1]
        sub_p, lane_p = sub[:pairs], lane[:pairs]
        ok = jnp.logical_and(up, right)
        corner = msg_recv[slot, jnp.where(ok, me - nx + 1, me)]
        corner = jnp.where(ok, corner, jnp.zeros_like(corner))
        corner = jnp.broadcast_to(corner, (pairs, LANES))
        corner = jnp.sum(jnp.where(lane_p == sub_p * T + T - 1, corner, 0.0), axis=1, keepdims=True)
        u_right = to_left(u, jnp.broadcast_to(corner, (pairs, LANES)))
        rate = wide(tau_ref[0:pairs])
        a2, b2 = shrink(
            grow[0] + rate * (row_send[slot, 0] - u), grow[1] + rate * (u_right - u), rate * ext_row_in[2]
        )
        grow[0] = jnp.where(up, a2, jnp.zeros_like(a2))
        grow[1] = jnp.where(up, b2, jnp.zeros_like(b2))
        u = col_recv[slot, 1]
        ok = jnp.logical_and(down, left)
        corner = msg_recv[slot, jnp.where(ok, me + nx - 1, me)]
        corner = jnp.where(ok, corner, jnp.zeros_like(corner))
        turn = jnp.where(sub == SUBS - 1, row8(corner, LANES), pltpu.roll(u, SUBS - 1, 0))
        u_down = jnp.where(within == T - 1, pltpu.roll(turn, T - 1, 1), pltpu.roll(u, LANES - 1, 1))
        rate = row8(tau_ref[0:1], LANES)
        for p in range(1, pairs):
            rate = jnp.where(group == p, row8(tau_ref[p:p + 1], LANES), rate)
        a2, b2 = shrink(
            gcol[0] + rate * (u_down - u), gcol[1] + rate * (col_send[slot, 0] - u), rate * ext_col_in[2]
        )
        gcol[0] = jnp.where(left, a2, jnp.zeros_like(a2))
        gcol[1] = jnp.where(left, b2, jnp.zeros_like(b2))

    def sweep(slot, closing):
        other = 1 - slot
        ghosts(slot)

        def problem(p, carry):
            sums_a, sums_b, first, last = carry
            tau = wide(row8(tau_ref[pl.ds(p, 1), :], LANES))
            sigma = wide(row8(sig_ref[pl.ds(p, 1), :], LANES))
            gb = ghost_flux(p)
            hc = pltpu.roll(col_recv[slot, 0], LANES - 1 - p * T, 1)
            acc_p = jnp.zeros((SUBS, C), f32)
            acc_d = jnp.zeros((SUBS, C), f32)
            pack_f, pack_l = ones, ones

            def dual(t, a2, above, b2, u):
                nonlocal acc_p, acc_d, pack_f, pack_l
                r2 = shortfall(p, t, a2, above, b2, gb)
                change = sigma * (r2 + (r2 - R[p, t]))
                u2 = u + change
                if closing:
                    acc_d = acc_d + r2 * r2
                    scatter(u_in, u2, p, t)
                    return
                acc_d = acc_d + change * change
                R[p, t] = r2
                U[p, t] = u2
                pack_f = pack_first(pack_f, u2, t)
                pack_l = pack_last(pack_l, u2, t)
                if t == 0:
                    row_send[other, 0, pl.ds(p, 1), :] = u2[0:1]
                if t == T - 1:
                    row_send[other, 1, pl.ds(p, 1), :] = u2[SUBS - 1:]

            u_first = u = U[p, 0]
            for t in range(T):
                if t < T - 1:
                    u_down = U[p, t + 1]
                else:
                    below = row8(row_recv[slot, 0, pl.ds(p, 1), :], C)
                    u_down = jnp.where(subw == SUBS - 1, below, pltpu.roll(u_first, SUBS - 1, 0))
                u_right = to_left(u, pltpu.roll(hc, (LANES - t) % LANES, 1))
                a, b = A[p, t], B[p, t]
                a2, b2 = shrink(a + tau * (u_down - u), b + tau * (u_right - u), tau * CO[t])
                if closing:
                    scatter(flow_in, a2, 0, p, t)
                    scatter(flow_in, b2, 1, p, t)
                else:
                    A[p, t] = a2
                    B[p, t] = b2
                    da, db = a2 - a, b2 - b
                    acc_p = acc_p + (da * da + db * db)
                if t:
                    dual(t, a2, above, b2, u)
                else:
                    a_first, b_first = a2, b2
                above, u = a2, u_down
            dual(0, a_first, above_first(above, p), b_first, u_first)

            def settle(sums, acc):
                part = jnp.sum(jnp.sum(acc, axis=0, keepdims=True), axis=1, keepdims=True)
                return jnp.where(group[0:1] == p, jnp.broadcast_to(part, (1, LANES)), sums)

            sums_b = settle(sums_b, acc_d)
            if closing:
                return sums_a, sums_b, first, last
            return settle(sums_a, acc_p), sums_b, place(first, pack_f, p), place(last, pack_l, p)

        start = (ones[0:1], ones[0:1], ones, ones)
        sums_a, sums_b, first, last = lax.fori_loop(0, pairs, problem, start)
        if not closing:
            col_send[other, 0] = first
            col_send[other, 1] = last
            start_all(halos(other))
        send_message(other, message(first, last, sums_a, sums_b))
        if closing:
            for copy in results:
                copy.start()
        else:
            wait_all(halos(other))
        wait_message(other)
        return total_rows(other)

    def turn(i, c):
        sums = sweep(lax.rem(i, 2), False)
        primal, dual = sums, pltpu.roll(sums, SUBS - pairs, 0)
        s = jnp.sqrt(jnp.sqrt((primal + epsilon) / (dual + epsilon)))
        tau_ref[...] = tau_ref[...] / s
        sig_ref[...] = sig_ref[...] * s
        return c

    lax.fori_loop(0, ITERS - 1, turn, 0)
    sums = sweep((ITERS - 1) % 2, True)
    cells = T * SUBS * C * n
    res_out[...] = sums / cells
    for copy in results:
        copy.wait()


def local(ny, nx, imbalance, flow, potential, cost):
    pairs, rows, cols = imbalance.shape
    T = rows // SUBS
    n = ny * nx
    assert 2 * pairs == SUBS and pairs * T <= LANES and T >= 4
    f32 = jnp.float32
    block = (pairs, T, SUBS, cols)
    packed = (SUBS, LANES)
    K = cols // LANES
    hbm = pl.BlockSpec(memory_space=pltpu.HBM)
    flow_out, u_out, res = pl.pallas_call(
        functools.partial(kernel, ny, nx),
        out_shape=(
            jax.ShapeDtypeStruct(flow.shape, f32),
            jax.ShapeDtypeStruct(potential.shape, f32),
            jax.ShapeDtypeStruct(packed, f32),
        ),
        in_specs=[hbm] * 4,
        out_specs=(hbm, hbm, pl.BlockSpec(memory_space=pltpu.VMEM)),
        scratch_shapes=[
            pltpu.VMEM((K, pairs, rows, LANES), f32), pltpu.VMEM((K, 2, pairs, rows, LANES), f32),
            pltpu.VMEM((K, pairs, rows, LANES), f32), pltpu.VMEM((K, rows, LANES), f32),
            pltpu.VMEM(block, f32), pltpu.VMEM(block, f32), pltpu.VMEM(block, f32), pltpu.VMEM(block, f32),
            pltpu.VMEM(block, f32), pltpu.VMEM(block[1:], f32),
            pltpu.VMEM(packed, f32), pltpu.VMEM(packed, f32),
            pltpu.VMEM((2, 2, pairs, cols), f32), pltpu.VMEM((2, 2) + packed, f32),
            pltpu.VMEM((2, 2, pairs, cols), f32), pltpu.VMEM((2, 2) + packed, f32),
            pltpu.VMEM((2, 1, LANES), f32), pltpu.VMEM((2, n, 1, LANES), f32),
            pltpu.VMEM((3, pairs, cols), f32), pltpu.VMEM((3,) + packed, f32),
            pltpu.VMEM((3, pairs, cols), f32), pltpu.VMEM((3,) + packed, f32),
            pltpu.VMEM((2, pairs, cols), f32), pltpu.VMEM((2,) + packed, f32),
            pltpu.SemaphoreType.DMA((2, 4)), pltpu.SemaphoreType.DMA((2, 4)),
            pltpu.SemaphoreType.DMA((2,)), pltpu.SemaphoreType.DMA((2,)),
            pltpu.SemaphoreType.DMA((2,)), pltpu.SemaphoreType.DMA((2,)),
            pltpu.SemaphoreType.DMA((4, K)), pltpu.SemaphoreType.DMA((2, K)),
        ],
        compiler_params=pltpu.CompilerParams(
            collective_id=0, has_side_effects=True, vmem_limit_bytes=48 * 1024 * 1024
        ),
    )(imbalance, flow, potential, cost)
    return flow_out, u_out, res[pairs:, 0]


def solution(mesh):
    placed = (P(None, "gy", "gx"), P(None, None, "gy", "gx"), P(None, "gy", "gx"), P("gy", "gx"))
    return jax.shard_map(
        functools.partial(local, mesh.shape["gy"], mesh.shape["gx"]),
        mesh=mesh,
        in_specs=placed,
        out_specs=(P(None, None, "gy", "gx"), P(None, "gy", "gx"), P()),
        check_vma=False,
    )
```

time: 891 us -> 104 us (0.12)
  blocking collectives: 484 us -> 0 us
  other arithmetic: 131 us -> 0 us
  local copies, waits for them, and re-layouts: 132 us -> 6.31 us
  starting transfers between devices: 118 us -> 0 us
  Pallas kernels: 0 us -> 97 us
  waiting for transfers between devices: 19.6 us -> 0 us
    psum x12 -> x0, blocking collectives: 484 us -> none  [the longest x11 442 us: iterate(): lax.psum((primal_local, dual_local), ('gy', 'gx'))]
    ppermute x50 -> x0, starting transfers between devices: 118 us -> none  [shifted(): lax.ppermute(value, axis, [(source, source + steps) for source in range(l...]
    pallas_call x0 -> x1, Pallas kernels: none -> 97 us  [local(): pl.pallas_call(functools.partial(kernel, ny, nx), out_shape=(jax.ShapeDty...]
    slice x75 -> x1, local copies, waits for them, and re-layouts: 88.3 us -> 0.63 us  [local(): return (flow_out, u_out, res[pairs:, 0])]
    reduce_sum x23 -> x0, other arithmetic: 76.7 us -> none  [the longest x11 59.3 us: iterate(): dual_local = jnp.sum(change * change, axis=(1, 2))]
    div x23 -> x0, other arithmetic: 42.8 us -> none  [the longest x11 42.2 us: shrink(): jnp.maximum(magnitude - threshold, 0.0) / jnp.maximum(magnitude, threshold)]
    broadcast_in_dim x27 -> x0, local copies, waits for them, and re-layouts: 32 us -> none  [the longest x13 16.2 us: divergence(): from_above[:, None, :]]
    ppermute x50 -> x0, waiting for transfers between devices: 19.6 us -> none  [shifted(): lax.ppermute(value, axis, [(source, source + steps) for source in range(l...]
  transfers between devices with their start and end apart: 50 -> 0, of which waited for: 11 -> 0; matrix products, arithmetic and copies ran while one was open for 11% -> 0% of each run, Pallas kernels for 0% -> 0%
where the time goes in v1:
time: 104 us
  Pallas kernels  97 us (93%)
  local copies, waits for them, and re-layouts  6.31 us (6%)
    pallas_call x1, Pallas kernels, local(): pl.pallas_call(functools.partial(kernel, ny, nx), out_shape=(jax.ShapeDty...  97 us
    unnamed x8, local copies, waits for them, and re-layouts  5.68 us

profile of v1, /device:TPU:0, one launch (start us, length us, event | category | flops | bytes accessed | tf_op | source)
XLA Modules:
  0.0 103.9 jit_solution(4777097964044046852)
XLA Ops:
  0.6 0.0 copy-start
  0.6 1.2 %copy-done = f32[4,128,512]{2,1,0:T(8,128)S(1)} copy-done((f32[4,128,512]{2,1,0:T(8,128)S(1)}, f32[4,128,512]{2,1,0:T(8,128)}, u32[]{:S(2)}) %copy-start) | copy-done | bytes 1048600
  1.9 0.0 copy-start.1
  1.9 1.2 %copy-done.1 = f32[4,128,512]{2,1,0:T(8,128)S(1)} copy-done((f32[4,128,512]{2,1,0:T(8,128)S(1)}, f32[4,128,512]{2,1,0:T(8,128)}, u32[]{:S(2)}) %copy-start.1) | copy-done | bytes 1048600
  3.1 0.0 copy-start.2
  3.1 0.9 copy-done.2
  4.0 97.0 %shard_map.67 = (f32[2,4,128,512]{3,2,1,0:T(8,128)S(1)}, f32[4,128,512]{2,1,0:T(8,128)S(1)}, f32[8,128]{1,0:T(8,128)S(1)}) custom-call(f32[4,128,512]{2,1,0:T(8,128)S(1)} %copy-done, f32[2,4,128,512]{3,2,1,0:T(8,128)} %flow_hbm.1, f32[4,128,512]{2,1,0:T(8,128)S(1)} %copy-done.1, f32[128,512]{1,0:T(8,128)S(1)} %copy-done.2), custom_call_target="tpu_custom_call" | custom-call | tf_op jit(solution)/shard_map/pallas_call | solution.py:400
  101.0 0.6 slice_reduce_fusion
  101.6 1.3 %copy.9 = f32[2,4,128,512]{3,2,1,0:T(8,128)} copy(f32[2,4,128,512]{3,2,1,0:T(8,128)S(1)} %get-tuple-element.12) | data formatting | bytes 4194304
  102.9 1.0 copy.10
Async XLA Ops:
  0.6 1.2 %copy-start = (f32[4,128,512]{2,1,0:T(8,128)S(1)}, f32[4,128,512]{2,1,0:T(8,128)}, u32[]{:S(2)}) copy-start(f32[4,128,512]{2,1,0:T(8,128)} %imb_hbm.1) | copy-start | bytes 3145732
  1.9 1.2 %copy-start.1 = (f32[4,128,512]{2,1,0:T(8,128)S(1)}, f32[4,128,512]{2,1,0:T(8,128)}, u32[]{:S(2)}) copy-start(f32[4,128,512]{2,1,0:T(8,128)} %u_hbm.1) | copy-start | bytes 3145732
  3.1 0.9 copy-start.2

commit v2 on v1

v2 whole, which is shorter than its diff:
```python
import functools

import jax
import jax.numpy as jnp
from jax import lax
from jax.experimental import pallas as pl
from jax.experimental.pallas import tpu as pltpu
from jax.sharding import PartitionSpec as P

ITERS = 12
LANES = 128
GROUPS = 4
SUBS = 8

initial_step = 0.35
epsilon = 1e-06
MESH = pl.DeviceIdType.MESH


def kernel(
    ny, nx,
    imb_hbm, flow_hbm, u_hbm, cost_hbm,
    flow_hbm_out, u_hbm_out, res_out,
    imb_in, flow_in, u_in, cost_in,
    A, B, U, R, IM, CO,
    tau_ref, sig_ref,
    row_send, col_send, row_recv, col_recv, msg_send, msg_recv,
    ext_row, ext_col, ext_row_in, ext_col_in, grow, gcol,
    halo_ssem, halo_rsem, msg_ssem, msg_rsem, ext_ssem, ext_rsem, in_sem, out_sem,
):
    pairs, T, _, C = A.shape
    n = ny * nx
    G = grow.shape[0]
    gp = pairs // G
    gy, gx = lax.axis_index("gy"), lax.axis_index("gx")
    me = gy * nx + gx
    up, down, left, right = gy > 0, gy < ny - 1, gx > 0, gx < nx - 1
    f32 = jnp.float32

    K = C // LANES

    def column(ref, k):
        return ref.at[(slice(None),) * (len(ref.shape) - 1) + (pl.ds(k * LANES, LANES),)]

    fetches = [
        pltpu.make_async_copy(column(src, k), dst.at[k], in_sem.at[i, k])
        for i, (src, dst) in enumerate(((cost_hbm, cost_in), (u_hbm, u_in), (flow_hbm, flow_in), (imb_hbm, imb_in)))
        for k in range(K)
    ]
    for copy in fetches:
        copy.start()

    def gather(ref, *index):
        rows = pl.ds(index[-1], SUBS, stride=T)
        return jnp.concatenate([ref[(k,) + index[:-1] + (rows, slice(None))] for k in range(K)], axis=1)

    def scatter(ref, value, *index):
        rows = pl.ds(index[-1], SUBS, stride=T)
        for k in range(K):
            ref[(k,) + index[:-1] + (rows, slice(None))] = value[:, k * LANES:(k + 1) * LANES]

    barrier = pltpu.get_barrier_semaphore()

    def coords(offset):
        other = lax.rem(me + offset, n)
        return (other // nx, lax.rem(other, nx))

    def greet(k, c):
        pl.semaphore_signal(barrier, inc=1, device_id=coords(k), device_id_type=MESH)
        return c

    lax.fori_loop(1, n, greet, 0)

    lane = lax.broadcasted_iota(jnp.int32, (SUBS, LANES), 1)
    sub = lax.broadcasted_iota(jnp.int32, (SUBS, LANES), 0)
    subw = lax.broadcasted_iota(jnp.int32, (SUBS, C), 0)
    group, within = lane // T, lax.rem(lane, T)
    lane1, within1 = lane[0:1], within[0:1]

    def wide(x):
        return jnp.concatenate([x] * (C // LANES), axis=1)

    def row8(x, width):
        return jnp.broadcast_to(x, (SUBS, width))

    def to_left(x, entering):
        r = pltpu.roll(x, C - 1, 1)
        lanes = lax.broadcasted_iota(jnp.int32, entering.shape, 1)
        tail = jnp.where(lanes == LANES - 1, entering, r[:, C - LANES:])
        return jnp.concatenate([r[:, : C - LANES], tail], axis=1)

    def to_right(x, entering):
        r = pltpu.roll(x, 1, 1)
        head = jnp.where(lane == 0, entering, r[:, :LANES])
        return jnp.concatenate([head, r[:, LANES:]], axis=1)

    def pack_first(acc, x, t):
        v = x[:, :LANES]
        return jnp.where(lane == t, pltpu.roll(v, t, 1) if t else v, acc)

    def pack_last(acc, x, t):
        v = pltpu.roll(x[:, C - LANES:], (t + 1) % LANES, 1)
        return jnp.where(lane == t, v, acc)

    def turned(x, by):
        return x if isinstance(by, int) and by == 0 else pltpu.roll(x, by, 1)

    def place(acc, packed, p):
        return jnp.where(group == p, turned(packed, p * T), acc)

    def remote(src, dst, ssem, rsem, where):
        return pltpu.make_async_remote_copy(
            src_ref=src, dst_ref=dst, send_sem=ssem, recv_sem=rsem, device_id=where, device_id_type=MESH
        )

    def halos(slot, g):
        rows = [
            (ok_to, ok_from, remote(row_send.at[slot, k, g], row_recv.at[slot, k, g], halo_ssem.at[slot, k, g], halo_rsem.at[slot, k, g], (gy + d, gx)))
            for k, d, ok_to, ok_from in ((0, -1, up, down), (1, 1, down, up))
        ]
        cols = [
            (ok_to, ok_from, remote(col_send.at[slot, k, g], col_recv.at[slot, k, g], halo_ssem.at[slot, 2 + k, g], halo_rsem.at[slot, 2 + k, g], (gy, gx + d)))
            for k, d, ok_to, ok_from in ((0, -1, left, right), (1, 1, right, left))
        ]
        return rows + cols

    def extras():
        return [
            (down, up, remote(ext_row, ext_row_in, ext_ssem.at[0], ext_rsem.at[0], (gy + 1, gx))),
            (right, left, remote(ext_col, ext_col_in, ext_ssem.at[1], ext_rsem.at[1], (gy, gx + 1))),
        ]

    def start_all(copies):
        for ok_to, _, copy in copies:
            @pl.when(ok_to)
            def _(copy=copy):
                copy.start()

    def wait_all(copies):
        for ok_to, ok_from, copy in copies:
            @pl.when(ok_from)
            def _(copy=copy):
                copy.wait_recv()

            @pl.when(ok_to)
            def _(copy=copy):
                copy.wait_send()

    def send_message(slot, g, row):
        msg_send[slot, g] = row
        msg_recv[slot, g, me] = row

        def send(j, c):
            y = jnp.where(gy < ny // 2, ny - 1 - j, j)
            for x in range(nx):
                @pl.when(jnp.logical_or(y != gy, gx != x))
                def _():
                    remote(
                        msg_send.at[slot, g], msg_recv.at[slot, g, me], msg_ssem.at[slot, g], msg_rsem.at[slot, g], (y, x)
                    ).start()
            return c

        lax.fori_loop(0, ny, send, 0)

    def wait_message(slot, g):
        whole = msg_recv.at[slot, g, pl.ds(0, n - 1)]
        pltpu.make_async_copy(whole, whole, msg_rsem.at[slot, g]).wait()
        pltpu.make_async_copy(whole, whole, msg_ssem.at[slot, g]).wait()

    def total_rows(slot, g):
        parts = [msg_recv[slot, g, k] for k in range(n)]
        while len(parts) > 1:
            parts = [sum(parts[k + 1:k + 2], parts[k]) for k in range(0, len(parts), 2)]
        total = row8(parts[0], LANES)
        pick = jnp.where(sub < gp, sub * T + 1, (sub - gp) * T + 2)
        return row8_lanes(jnp.sum(jnp.where(lane == pick, total, 0.0), axis=1, keepdims=True))

    def each(body, init):
        return lax.fori_loop(0, gp, body, init) if gp > 1 else body(0, init)

    def row8_lanes(x):
        return jnp.broadcast_to(x, (SUBS, LANES))

    def message(first, last, sums_a, sums_b):
        return jnp.where(
            within1 == T - 1, first[SUBS - 1:SUBS],
            jnp.where(within1 == 0, last[0:1], jnp.where(within1 == 1, sums_a, sums_b)),
        )

    ones = jnp.ones((SUBS, LANES), f32)
    for copy in fetches:
        copy.wait()
    for t in range(T):
        CO[t] = gather(cost_in, t)

    def load(g, c):
        def problem(p, carry):
            packs = [ones] * 5
            q = g * gp + p
            for t in range(T):
                a, b = gather(flow_in, 0, q, t), gather(flow_in, 1, q, t)
                u = gather(u_in, q, t)
                A[q, t] = a
                B[q, t] = b
                U[q, t] = u
                IM[q, t] = gather(imb_in, q, t)
                packs[0] = pack_first(packs[0], u, t)
                for k, x in ((1, u), (2, a), (3, b), (4, CO[t])):
                    packs[k] = pack_last(packs[k], x, t)
                if t == 0:
                    row_send[0, 0, g, pl.ds(p, 1), :] = u[0:1]
                if t == T - 1:
                    row_send[0, 1, g, pl.ds(p, 1), :] = u[SUBS - 1:]
                    ext_row[0, g, pl.ds(p, 1), :] = a[SUBS - 1:]
                    ext_row[1, g, pl.ds(p, 1), :] = b[SUBS - 1:]
                    ext_row[2, g, pl.ds(p, 1), :] = CO[t][SUBS - 1:]
            return tuple(place(c, x, p) for c, x in zip(carry, packs))

        first, last, last_a, last_b, last_c = each(problem, (ones,) * 5)
        col_send[0, 0, g] = first
        col_send[0, 1, g] = last
        ext_col[0, g] = last_a
        ext_col[1, g] = last_b
        ext_col[2, g] = last_c
        return c

    lax.fori_loop(0, G, load, 0)
    tau_ref[...] = jnp.full(tau_ref.shape, initial_step, f32)
    sig_ref[...] = jnp.full(sig_ref.shape, initial_step, f32)

    for missing, refs in (
        (jnp.logical_not(down), [row_recv.at[s, 0] for s in range(2)]),
        (jnp.logical_not(up), [row_recv.at[s, 1] for s in range(2)] + [ext_row_in]),
        (jnp.logical_not(right), [col_recv.at[s, 0] for s in range(2)]),
        (jnp.logical_not(left), [col_recv.at[s, 1] for s in range(2)] + [ext_col_in]),
    ):
        @pl.when(missing)
        def _(refs=refs):
            for ref in refs:
                ref[...] = jnp.zeros(ref.shape, f32)

    pl.semaphore_wait(barrier, n - 1)
    start_all(extras())

    def announce(g, c):
        start_all(halos(0, g))
        send_message(0, g, message(col_send[0, 0, g], col_send[0, 1, g], ones[0:1], ones[0:1]))
        return c

    lax.fori_loop(0, G, announce, 0)
    wait_all(extras())
    for k in range(2):
        for g in range(G):
            grow[g, k] = ext_row_in[k, g]
            gcol[g, k] = ext_col_in[k, g]

    def above_first(a_last, g, p):
        ghost = row8(grow[g, 0, pl.ds(p, 1), :], C)
        return jnp.where(subw == 0, ghost, pltpu.roll(a_last, 1, 0))

    def shortfall(p, t, a, a_above, b, gb):
        b_left = to_right(b, pltpu.roll(gb, (LANES - t) % LANES, 1))
        return ((a - a_above) + (b - b_left)) - IM[p, t]

    def ghost_flux(g, p):
        return turned(gcol[g, 1], (LANES - p * T) % LANES)

    def begin(g, c):
        def problem(p, c):
            q = g * gp + p
            gb = ghost_flux(g, p)
            for t in range(T):
                above = A[q, t - 1] if t else above_first(A[q, T - 1], g, p)
                R[q, t] = shortfall(q, t, A[q, t], above, B[q, t], gb)
            return c

        return each(problem, c)

    lax.fori_loop(0, G, begin, 0)

    results = [
        pltpu.make_async_copy(src.at[k], column(dst, k), out_sem.at[i, k])
        for i, (src, dst) in enumerate(((flow_in, flow_hbm_out), (u_in, u_hbm_out)))
        for k in range(K)
    ]

    def shrink(va, vb, t):
        f = jnp.maximum(1.0 - t * lax.rsqrt(va * va + vb * vb), 0.0)
        return f * va, f * vb

    def ghosts(slot, g):
        u = row_recv[slot, 1, g]
        sub_p, lane_p = sub[:gp], lane[:gp]
        ok = jnp.logical_and(up, right)
        corner = msg_recv[slot, g, jnp.where(ok, me - nx + 1, me)]
        corner = jnp.where(ok, corner, jnp.zeros_like(corner))
        corner = jnp.broadcast_to(corner, (gp, LANES))
        corner = jnp.sum(jnp.where(lane_p == sub_p * T + T - 1, corner, 0.0), axis=1, keepdims=True)
        u_right = to_left(u, jnp.broadcast_to(corner, (gp, LANES)))
        rate = wide(tau_ref[g, 0:gp])
        a2, b2 = shrink(
            grow[g, 0] + rate * (row_send[slot, 0, g] - u), grow[g, 1] + rate * (u_right - u), rate * ext_row_in[2, g]
        )
        grow[g, 0] = jnp.where(up, a2, jnp.zeros_like(a2))
        grow[g, 1] = jnp.where(up, b2, jnp.zeros_like(b2))
        u = col_recv[slot, 1, g]
        ok = jnp.logical_and(down, left)
        corner = msg_recv[slot, g, jnp.where(ok, me + nx - 1, me)]
        corner = jnp.where(ok, corner, jnp.zeros_like(corner))
        turn = jnp.where(sub == SUBS - 1, row8(corner, LANES), pltpu.roll(u, SUBS - 1, 0))
        u_down = jnp.where(within == T - 1, pltpu.roll(turn, T - 1, 1), pltpu.roll(u, LANES - 1, 1))
        rate = row8(tau_ref[g, 0:1], LANES)
        for p in range(1, gp):
            rate = jnp.where(group == p, row8(tau_ref[g, p:p + 1], LANES), rate)
        a2, b2 = shrink(
            gcol[g, 0] + rate * (u_down - u), gcol[g, 1] + rate * (col_send[slot, 0, g] - u), rate * ext_col_in[2, g]
        )
        gcol[g, 0] = jnp.where(left, a2, jnp.zeros_like(a2))
        gcol[g, 1] = jnp.where(left, b2, jnp.zeros_like(b2))

    def sweep(i, g, slot, closing):
        other = 1 - slot
        wait_all(halos(slot, g))
        wait_message(slot, g)
        sums = total_rows(slot, g)
        primal, dual_sums = sums, pltpu.roll(sums, SUBS - gp, 0)
        s = jnp.sqrt(jnp.sqrt((primal + epsilon) / (dual_sums + epsilon)))
        s = jnp.where(i == 0, 1.0, s)
        tau_ref[g] = tau_ref[g] / s
        sig_ref[g] = sig_ref[g] * s
        ghosts(slot, g)

        def problem(p, carry):
            sums_a, sums_b, first, last = carry
            q = g * gp + p
            tau = wide(row8(tau_ref[g, pl.ds(p, 1), :], LANES))
            sigma = wide(row8(sig_ref[g, pl.ds(p, 1), :], LANES))
            gb = ghost_flux(g, p)
            hc = pltpu.roll(col_recv[slot, 0, g], LANES - 1 - p * T, 1)
            acc_p = jnp.zeros((SUBS, C), f32)
            acc_d = jnp.zeros((SUBS, C), f32)
            pack_f, pack_l = ones, ones

            def dual(t, a2, above, b2, u):
                nonlocal acc_p, acc_d, pack_f, pack_l
                r2 = shortfall(q, t, a2, above, b2, gb)
                change = sigma * (r2 + (r2 - R[q, t]))
                u2 = u + change
                if closing:
                    acc_d = acc_d + r2 * r2
                    scatter(u_in, u2, q, t)
                    return
                acc_d = acc_d + change * change
                R[q, t] = r2
                U[q, t] = u2
                pack_f = pack_first(pack_f, u2, t)
                pack_l = pack_last(pack_l, u2, t)
                if t == 0:
                    row_send[other, 0, g, pl.ds(p, 1), :] = u2[0:1]
                if t == T - 1:
                    row_send[other, 1, g, pl.ds(p, 1), :] = u2[SUBS - 1:]

            u_first = u = U[q, 0]
            for t in range(T):
                if t < T - 1:
                    u_down = U[q, t + 1]
                else:
                    below = row8(row_recv[slot, 0, g, pl.ds(p, 1), :], C)
                    u_down = jnp.where(subw == SUBS - 1, below, pltpu.roll(u_first, SUBS - 1, 0))
                u_right = to_left(u, pltpu.roll(hc, (LANES - t) % LANES, 1))
                a, b = A[q, t], B[q, t]
                a2, b2 = shrink(a + tau * (u_down - u), b + tau * (u_right - u), tau * CO[t])
                if closing:
                    scatter(flow_in, a2, 0, q, t)
                    scatter(flow_in, b2, 1, q, t)
                else:
                    A[q, t] = a2
                    B[q, t] = b2
                    da, db = a2 - a, b2 - b
                    acc_p = acc_p + (da * da + db * db)
                if t:
                    dual(t, a2, above, b2, u)
                else:
                    a_first, b_first = a2, b2
                above, u = a2, u_down
            dual(0, a_first, above_first(above, g, p), b_first, u_first)

            def settle(sums, acc):
                part = jnp.sum(jnp.sum(acc, axis=0, keepdims=True), axis=1, keepdims=True)
                return jnp.where(group[0:1] == p, jnp.broadcast_to(part, (1, LANES)), sums)

            sums_b = settle(sums_b, acc_d)
            if closing:
                return sums_a, sums_b, first, last
            return settle(sums_a, acc_p), sums_b, place(first, pack_f, p), place(last, pack_l, p)

        start = (ones[0:1], ones[0:1], ones, ones)
        sums_a, sums_b, first, last = each(problem, start)
        if not closing:
            col_send[other, 0, g] = first
            col_send[other, 1, g] = last
        send_message(other, g, message(first, last, sums_a, sums_b))
        if not closing:
            start_all(halos(other, g))

    def turn(i, c):
        def one(g, c):
            sweep(i, g, lax.rem(i, 2), False)
            return c

        return lax.fori_loop(0, G, one, c)

    lax.fori_loop(0, ITERS - 1, turn, 0)
    slot = (ITERS - 1) % 2

    def close(g, c):
        sweep(ITERS - 1, g, slot, True)
        return c

    lax.fori_loop(0, G, close, 0)
    for copy in results:
        copy.start()
    cells = T * SUBS * C * n
    for g in range(G):
        wait_message(1 - slot, g)
        res_out[g] = total_rows(1 - slot, g) / cells
    for copy in results:
        copy.wait()


def local(ny, nx, imbalance, flow, potential, cost):
    pairs, rows, cols = imbalance.shape
    T = rows // SUBS
    n = ny * nx
    assert 2 * pairs <= SUBS and pairs * T <= LANES and T >= 4
    G = GROUPS if pairs % GROUPS == 0 else 1
    gp = pairs // G
    f32 = jnp.float32
    block = (pairs, T, SUBS, cols)
    packed = (SUBS, LANES)
    K = cols // LANES
    hbm = pl.BlockSpec(memory_space=pltpu.HBM)
    flow_out, u_out, res = pl.pallas_call(
        functools.partial(kernel, ny, nx),
        out_shape=(
            jax.ShapeDtypeStruct(flow.shape, f32),
            jax.ShapeDtypeStruct(potential.shape, f32),
            jax.ShapeDtypeStruct((G,) + packed, f32),
        ),
        in_specs=[hbm] * 4,
        out_specs=(hbm, hbm, pl.BlockSpec(memory_space=pltpu.VMEM)),
        scratch_shapes=[
            pltpu.VMEM((K, pairs, rows, LANES), f32), pltpu.VMEM((K, 2, pairs, rows, LANES), f32),
            pltpu.VMEM((K, pairs, rows, LANES), f32), pltpu.VMEM((K, rows, LANES), f32),
            pltpu.VMEM(block, f32), pltpu.VMEM(block, f32), pltpu.VMEM(block, f32), pltpu.VMEM(block, f32),
            pltpu.VMEM(block, f32), pltpu.VMEM(block[1:], f32),
            pltpu.VMEM((G,) + packed, f32), pltpu.VMEM((G,) + packed, f32),
            pltpu.VMEM((2, 2, G, gp, cols), f32), pltpu.VMEM((2, 2, G) + packed, f32),
            pltpu.VMEM((2, 2, G, gp, cols), f32), pltpu.VMEM((2, 2, G) + packed, f32),
            pltpu.VMEM((2, G, 1, LANES), f32), pltpu.VMEM((2, G, n, 1, LANES), f32),
            pltpu.VMEM((3, G, gp, cols), f32), pltpu.VMEM((3, G) + packed, f32),
            pltpu.VMEM((3, G, gp, cols), f32), pltpu.VMEM((3, G) + packed, f32),
            pltpu.VMEM((G, 2, gp, cols), f32), pltpu.VMEM((G, 2) + packed, f32),
            pltpu.SemaphoreType.DMA((2, 4, G)), pltpu.SemaphoreType.DMA((2, 4, G)),
            pltpu.SemaphoreType.DMA((2, G)), pltpu.SemaphoreType.DMA((2, G)),
            pltpu.SemaphoreType.DMA((2,)), pltpu.SemaphoreType.DMA((2,)),
            pltpu.SemaphoreType.DMA((4, K)), pltpu.SemaphoreType.DMA((2, K)),
        ],
        compiler_params=pltpu.CompilerParams(
            collective_id=0, has_side_effects=True, vmem_limit_bytes=48 * 1024 * 1024
        ),
    )(imbalance, flow, potential, cost)
    return flow_out, u_out, res[:, gp:2 * gp, 0].reshape(pairs)


def solution(mesh):
    placed = (P(None, "gy", "gx"), P(None, None, "gy", "gx"), P(None, "gy", "gx"), P("gy", "gx"))
    return jax.shard_map(
        functools.partial(local, mesh.shape["gy"], mesh.shape["gx"]),
        mesh=mesh,
        in_specs=placed,
        out_specs=(P(None, None, "gy", "gx"), P(None, "gy", "gx"), P()),
        check_vma=False,
    )
```

time: 104 us -> 82.2 us (0.79)
  Pallas kernels: 97 us -> 75 us
    pallas_call x1, Pallas kernels: 97 us -> 75 us  [local(): pl.pallas_call(functools.partial(kernel, ny, nx), out_shape=(jax.ShapeDty...]
where the time goes in v2:
time: 82.2 us; the launch traced here: 82 us
  Pallas kernels  75 us (91%)
  local copies, waits for them, and re-layouts  6.31 us (8%)
    pallas_call x1, Pallas kernels, local(): pl.pallas_call(functools.partial(kernel, ny, nx), out_shape=(jax.ShapeDty...  75 us
    unnamed x8, local copies, waits for them, and re-layouts  5.68 us

profile of v2, /device:TPU:0, one launch (start us, length us, event | category | flops | bytes accessed | tf_op | source)
XLA Modules:
  0.0 82.0 jit_solution(10789630012726252260)
XLA Ops:
  0.6 0.0 copy-start
  0.6 1.2 %copy-done = f32[4,128,512]{2,1,0:T(8,128)S(1)} copy-done((f32[4,128,512]{2,1,0:T(8,128)S(1)}, f32[4,128,512]{2,1,0:T(8,128)}, u32[]{:S(2)}) %copy-start) | copy-done | bytes 1048600
  1.9 0.0 copy-start.1
  1.9 1.2 %copy-done.1 = f32[4,128,512]{2,1,0:T(8,128)S(1)} copy-done((f32[4,128,512]{2,1,0:T(8,128)S(1)}, f32[4,128,512]{2,1,0:T(8,128)}, u32[]{:S(2)}) %copy-start.1) | copy-done | bytes 1048600
  3.1 0.0 copy-start.2
  3.1 0.9 %copy-done.2 = f32[128,512]{1,0:T(8,128)S(1)} copy-done((f32[128,512]{1,0:T(8,128)S(1)}, f32[128,512]{1,0:T(8,128)}, u32[]{:S(2)}) %copy-start.2) | copy-done | bytes 262168
  4.0 75.0 %shard_map.67 = (f32[2,4,128,512]{3,2,1,0:T(8,128)S(1)}, f32[4,128,512]{2,1,0:T(8,128)S(1)}, f32[4,8,128]{2,1,0:T(8,128)S(1)}) custom-call(f32[4,128,512]{2,1,0:T(8,128)S(1)} %copy-done, f32[2,4,128,512]{3,2,1,0:T(8,128)} %flow_hbm.1, f32[4,128,512]{2,1,0:T(8,128)S(1)} %copy-done.1, f32[128,512]{1,0:T(8,128)S(1)} %copy-done.2), custom_call_target="tpu_custom_call" | custom-call | tf_op jit(solution)/shard_map/pallas_call | solution.py:443
  79.1 0.6 slice_reduce_fusion
  79.7 1.3 %copy.9 = f32[2,4,128,512]{3,2,1,0:T(8,128)} copy(f32[2,4,128,512]{3,2,1,0:T(8,128)S(1)} %get-tuple-element.12) | data formatting | bytes 4194304
  81.0 1.0 %copy.10 = f32[4,128,512]{2,1,0:T(8,128)} copy(f32[4,128,512]{2,1,0:T(8,128)S(1)} %get-tuple-element.13) | data formatting | bytes 2097152
Async XLA Ops:
  0.6 1.2 %copy-start = (f32[4,128,512]{2,1,0:T(8,128)S(1)}, f32[4,128,512]{2,1,0:T(8,128)}, u32[]{:S(2)}) copy-start(f32[4,128,512]{2,1,0:T(8,128)} %imb_hbm.1) | copy-start | bytes 3145732
  1.9 1.2 %copy-start.1 = (f32[4,128,512]{2,1,0:T(8,128)S(1)}, f32[4,128,512]{2,1,0:T(8,128)}, u32[]{:S(2)}) copy-start(f32[4,128,512]{2,1,0:T(8,128)} %u_hbm.1) | copy-start | bytes 3145732
  3.1 0.9 %copy-start.2 = (f32[128,512]{1,0:T(8,128)S(1)}, f32[128,512]{1,0:T(8,128)}, u32[]{:S(2)}) copy-start(f32[128,512]{1,0:T(8,128)} %cost_hbm.1) | copy-start | bytes 786436

commit v3 on v2

--- a/solution.py
+++ b/solution.py
@@ -150,7 +150,7 @@
         msg_send[slot, g] = row
         msg_recv[slot, g, me] = row
 
-        def send(j, c):
+        for j in range(ny):
             y = jnp.where(gy < ny // 2, ny - 1 - j, j)
             for x in range(nx):
                 @pl.when(jnp.logical_or(y != gy, gx != x))
@@ -158,9 +158,6 @@
                     remote(
                         msg_send.at[slot, g], msg_recv.at[slot, g, me], msg_ssem.at[slot, g], msg_rsem.at[slot, g], (y, x)
                     ).start()
-            return c
-
-        lax.fori_loop(0, ny, send, 0)
 
     def wait_message(slot, g):
         whole = msg_recv.at[slot, g, pl.ds(0, n - 1)]
@@ -242,9 +239,19 @@
     pl.semaphore_wait(barrier, n - 1)
     start_all(extras())
 
+    def corners(g):
+        return [
+            (ok_to, ok_from, remote(msg_send.at[0, g], msg_recv.at[0, g, me], msg_ssem.at[2 + k, g], msg_rsem.at[2 + k, g], (gy + dy, gx + dx)))
+            for k, dy, dx, ok_to, ok_from in (
+                (0, -1, 1, jnp.logical_and(up, right), jnp.logical_and(down, left)),
+                (1, 1, -1, jnp.logical_and(down, left), jnp.logical_and(up, right)),
+            )
+        ]
+
     def announce(g, c):
-        start_all(halos(0, g))
-        send_message(0, g, message(col_send[0, 0, g], col_send[0, 1, g], ones[0:1], ones[0:1]))
+        row = message(col_send[0, 0, g], col_send[0, 1, g], ones[0:1], ones[0:1])
+        msg_send[0, g] = row
+        start_all(halos(0, g) + corners(g))
         return c
 
     lax.fori_loop(0, G, announce, 0)
@@ -277,6 +284,12 @@
         return each(problem, c)
 
     lax.fori_loop(0, G, begin, 0)
+
+    def settled(g, c):
+        wait_all(halos(0, g) + corners(g))
+        return c
+
+    lax.fori_loop(0, G, settled, 0)
 
     results = [
         pltpu.make_async_copy(src.at[k], column(dst, k), out_sem.at[i, k])
@@ -318,16 +331,17 @@
         gcol[g, 0] = jnp.where(left, a2, jnp.zeros_like(a2))
         gcol[g, 1] = jnp.where(left, b2, jnp.zeros_like(b2))
 
-    def sweep(i, g, slot, closing):
-        other = 1 - slot
+    def adapt(slot, g):
         wait_all(halos(slot, g))
         wait_message(slot, g)
         sums = total_rows(slot, g)
         primal, dual_sums = sums, pltpu.roll(sums, SUBS - gp, 0)
         s = jnp.sqrt(jnp.sqrt((primal + epsilon) / (dual_sums + epsilon)))
-        s = jnp.where(i == 0, 1.0, s)
         tau_ref[g] = tau_ref[g] / s
         sig_ref[g] = sig_ref[g] * s
+
+    def sweep(g, slot, closing):
+        other = 1 - slot
         ghosts(slot, g)
 
         def problem(p, carry):
@@ -404,8 +418,14 @@
             start_all(halos(other, g))
 
     def turn(i, c):
+        slot = lax.rem(i, 2)
+
         def one(g, c):
-            sweep(i, g, lax.rem(i, 2), False)
+            @pl.when(i > 0)
+            def _():
+                adapt(slot, g)
+
+            sweep(g, slot, False)
             return c
 
         return lax.fori_loop(0, G, one, c)
@@ -414,7 +434,8 @@
     slot = (ITERS - 1) % 2
 
     def close(g, c):
-        sweep(ITERS - 1, g, slot, True)
+        adapt(slot, g)
+        sweep(g, slot, True)
         return c
 
     lax.fori_loop(0, G, close, 0)
@@ -462,14 +483,14 @@
             pltpu.VMEM((3, G, gp, cols), f32), pltpu.VMEM((3, G) + packed, f32),
             pltpu.VMEM((G, 2, gp, cols), f32), pltpu.VMEM((G, 2) + packed, f32),
             pltpu.SemaphoreType.DMA((2, 4, G)), pltpu.SemaphoreType.DMA((2, 4, G)),
-            pltpu.SemaphoreType.DMA((2, G)), pltpu.SemaphoreType.DMA((2, G)),
+            pltpu.SemaphoreType.DMA((4, G)), pltpu.SemaphoreType.DMA((4, G)),
             pltpu.SemaphoreType.DMA((2,)), pltpu.SemaphoreType.DMA((2,)),
             pltpu.SemaphoreType.DMA((4, K)), pltpu.SemaphoreType.DMA((2, K)),
         ],
         compiler_params=pltpu.CompilerParams(
             collective_id=0, has_side_effects=True, vmem_limit_bytes=48 * 1024 * 1024
         ),
-    )(imbalance, flow, potential, cost)
+    )(*(pltpu.with_memory_space_constraint(x, pltpu.HBM) for x in (imbalance, flow, potential, cost)))
     return flow_out, u_out, res[:, gp:2 * gp, 0].reshape(pairs)
 
 

time: 82.2 us -> 77.9 us (0.948)
  local copies, waits for them, and re-layouts: 6.31 us -> 2.91 us
    unnamed x8 -> x2, local copies, waits for them, and re-layouts: 5.68 us -> 2.29 us
    pallas_call x1, Pallas kernels: 75 us -> 74.2 us  [local(): pl.pallas_call(functools.partial(kernel, ny, nx), out_shape=(jax.ShapeDty...]
where the time goes in v3:
time: 77.9 us; the launch traced here: 77.7 us
  Pallas kernels  74.2 us (95%)
  local copies, waits for them, and re-layouts  2.91 us (4%)
    pallas_call x1, Pallas kernels, local(): pl.pallas_call(functools.partial(kernel, ny, nx), out_shape=(jax.ShapeDty...  74.2 us
    unnamed x2, local copies, waits for them, and re-layouts  2.29 us

profile of v3, /device:TPU:0, one launch (start us, length us, event | category | flops | bytes accessed | tf_op | source)
XLA Modules:
  0.0 77.7 jit_solution(5154616623095843889)
XLA Ops:
  0.6 74.2 %shard_map.67 = (f32[2,4,128,512]{3,2,1,0:T(8,128)S(1)}, f32[4,128,512]{2,1,0:T(8,128)S(1)}, f32[4,8,128]{2,1,0:T(8,128)S(1)}) custom-call(f32[4,128,512]{2,1,0:T(8,128)} %imb_hbm.1, f32[2,4,128,512]{3,2,1,0:T(8,128)} %flow_hbm.1, f32[4,128,512]{2,1,0:T(8,128)} %u_hbm.1, f32[128,512]{1,0:T(8,128)} %cost_hbm.1), custom_call_target="tpu_custom_call" | custom-call | tf_op jit(solution)/shard_map/pallas_call | solution.py:464
  74.8 0.6 slice_reduce_fusion
  75.5 1.3 %copy.9 = f32[2,4,128,512]{3,2,1,0:T(8,128)} copy(f32[2,4,128,512]{3,2,1,0:T(8,128)S(1)} %get-tuple-element.12) | data formatting | bytes 4194304
  76.8 1.0 %copy.10 = f32[4,128,512]{2,1,0:T(8,128)} copy(f32[4,128,512]{2,1,0:T(8,128)S(1)} %get-tuple-element.13) | data formatting | bytes 2097152
